TPU v7x, 32 devices: a whole 2x2x4 slice. The times are simulated.
32 devices in a mesh: tm: 4 (over y, core), space: 8 (over z, x).
Axes of the slice: x: 2, y: 2, z: 4, core: 2. Of those that a mesh axis runs over, the one named last changes fastest.
Arguments:
- state: bfloat16 [4, 4096, 137], P('tm', 'space'), may hold values from -6 to 6
- obs_start: int32 [16384], P(('tm', 'space')), may hold values from 0 to 4095, as said below
- foot_weight: bfloat16 [16384, 8], P(('tm', 'space')), may hold values from 0.019897461 to 0.29882812
- obs_slot: int32 [16384], P(('tm', 'space')), may hold values from 0 to 2
- obs_frac: float32 [16384], P(('tm', 'space')), may hold values from 0 to 1
- live_count: int32 [4, 8], P('tm', 'space'), may hold values from 64 to 512
- obs_values: float32 [16384, 128], P(('tm', 'space')), may hold values from -6 to 6
- jacobian: bfloat16 [137, 128], replicated, may hold values from -0.5 to 0.5
- inv_var: float32 [128], replicated, may hold values from 0.25 to 4
Outputs:
- departures: float32 [16384, 128], P(('tm', 'space'))
- adjoint: float32 [4, 4096, 137], P('tm', 'space')
Inputs may be any that keep to these rules, and one draw needn't show every extreme that they name: `obs_start`: on the devices of space index s, every observation's footprint columns lie within 256 columns of tile s, that is within s * 512 - 256 .. (s + 1) * 512 + 255 taken modulo 4096. `live_count`: rows at or beyond a device's count are padding.
All inputs are finite; a program needn't handle non-finite values.
Results may differ from a plain program's by a relative error of at most 0.008.
Values may be sent and summed in bfloat16 or wider, within the bound.
A program may use at most 64 MiB of HBM per device.

v0:
```python
import jax
import jax.numpy as jnp
from jax import lax
from jax.sharding import PartitionSpec as P

block_rows = 128


def with_halo(cells, sides, width):
    for axis, dim in sides:
        count = lax.axis_size(axis)
        head = lax.slice_in_dim(cells, 0, width, axis=dim)
        tail = lax.slice_in_dim(cells, cells.shape[dim] - width, cells.shape[dim], axis=dim)
        cells = jnp.concatenate(
            [
                lax.ppermute(tail, axis, [(i, (i + 1) % count) for i in range(count)]),
                cells,
                lax.ppermute(head, axis, [((i + 1) % count, i) for i in range(count)]),
            ],
            axis=dim,
        )
    return cells


def shifted(block, axis, distance):
    devices = range(lax.axis_size(axis))
    route = [((i - distance) % len(devices), i) for i in devices]
    return lax.ppermute(block, axis, route)


def footprint_matrix(starts, weights, tile, cols_dev, halo_w, total_cols):
    local = jnp.mod(starts - tile * cols_dev + halo_w, total_cols)
    width = cols_dev + 2 * halo_w
    place = lax.broadcasted_iota(jnp.int32, (starts.shape[0], width), 1)
    offset = place - local[:, None]
    matrix = jnp.zeros((starts.shape[0], width), jnp.float32)
    for column in range(weights.shape[1]):
        matrix = matrix + jnp.where(
            offset == column, weights[:, column : column + 1].astype(jnp.float32), 0.0
        )
    return matrix.astype(jnp.bfloat16)


def time_weight(slot, frac, held):
    return jnp.where(slot == held, 1.0 - frac, 0.0) + jnp.where(slot + 1 == held, frac, 0.0)


def gather_slot(interp, foot_mat, wide, weight, blocks):

    def gather_one_block(index, total):
        first = index * block_rows
        rows = lax.dynamic_slice_in_dim(foot_mat, first, block_rows, 0)
        part = jnp.dot(rows, wide, preferred_element_type=jnp.float32)
        scale = lax.dynamic_slice_in_dim(weight, first, block_rows, 0)
        current = lax.dynamic_slice_in_dim(total, first, block_rows, 0)
        return lax.dynamic_update_slice_in_dim(total, current + scale[:, None] * part, first, 0)

    return lax.fori_loop(0, blocks, gather_one_block, interp)


def spread_slot(foot_mat, back, weight, blocks, width, levels):

    def spread_one_block(index, total):
        first = index * block_rows
        rows = lax.dynamic_slice_in_dim(foot_mat, first, block_rows, 0)
        scale = lax.dynamic_slice_in_dim(weight, first, block_rows, 0)
        source = lax.dynamic_slice_in_dim(back, first, block_rows, 0)
        part = (scale[:, None] * source.astype(jnp.float32)).astype(jnp.bfloat16)
        return total + lax.dot_general(
            rows, part, (((0,), (0,)), ((), ())), preferred_element_type=jnp.float32
        )

    return lax.fori_loop(0, blocks, spread_one_block, jnp.zeros((width, levels), jnp.float32))


def fold_rims(wide, from_left, from_right, halo_w, cols_dev):
    core = wide[halo_w : halo_w + cols_dev]
    core = core.at[:halo_w].add(from_left)
    return core.at[cols_dev - halo_w :].add(from_right)


def body(
    state, obs_start, foot_weight, obs_slot, obs_frac, live_count, obs_values, jacobian, inv_var
):
    own = state[0]
    cols_dev, levels = own.shape
    halo_w = cols_dev // 2
    width = cols_dev + 2 * halo_w
    slots = lax.axis_size("tm")
    tile = lax.axis_index("space")
    turn = lax.axis_index("tm")
    total_cols = cols_dev * lax.axis_size("space")
    count = live_count[0, 0]
    blocks = (count + block_rows - 1) // block_rows
    obs_rows = obs_start.shape[0]
    foot_mat = footprint_matrix(obs_start, foot_weight, tile, cols_dev, halo_w, total_cols)
    interp = jnp.zeros((obs_rows, levels), jnp.float32)

    def forward_weight(step):
        return time_weight(obs_slot, obs_frac, jnp.mod(turn - step, slots))

    def backward_weight(step):
        return time_weight(obs_slot, obs_frac, jnp.mod(turn + slots - 1 - step, slots))

    wide_own = with_halo(own, (("space", 0),), halo_w)
    interp = gather_slot(interp, foot_mat, wide_own, forward_weight(0), blocks)

    def forward_wide(step, carry):
        wide, total = carry
        wide = shifted(wide, "tm", 1)
        return (wide, gather_slot(total, foot_mat, wide, forward_weight(step), blocks))

    carried, interp = lax.fori_loop(1, slots, forward_wide, (wide_own, interp))
    projected = jnp.dot(interp.astype(jnp.bfloat16), jacobian, preferred_element_type=jnp.float32)
    row_live = jnp.arange(obs_rows, dtype=jnp.int32) < count
    departures = jnp.where(row_live[:, None], obs_values - projected, 0.0)
    scaled = (departures * inv_var[None, :]).astype(jnp.bfloat16)
    back = jnp.dot(scaled, jacobian.T, preferred_element_type=jnp.float32).astype(jnp.bfloat16)

    def backward_wide(step, total):
        total = shifted(total, "tm", 1)
        return total + spread_slot(foot_mat, back, backward_weight(step), blocks, width, levels)

    start_sum = spread_slot(foot_mat, back, backward_weight(0), blocks, width, levels)
    wide_sum = lax.fori_loop(1, slots, backward_wide, start_sum)
    from_right = shifted(wide_sum[:halo_w], "space", -1)
    from_left = shifted(wide_sum[halo_w + cols_dev :], "space", 1)
    adjoint = fold_rims(wide_sum, from_left, from_right, halo_w, cols_dev)
    return (departures, adjoint[None])


def solution(mesh):
    return jax.shard_map(
        body,
        mesh=mesh,
        in_specs=(
            P("tm", "space", None),
            P(("tm", "space")),
            P(("tm", "space"), None),
            P(("tm", "space")),
            P(("tm", "space")),
            P("tm", "space"),
            P(("tm", "space"), None),
            P(),
            P(),
        ),
        out_specs=(P(("tm", "space"), None), P("tm", "space", None)),
        check_vma=False,
    )
```

profile of v0, /device:TPU:0, one launch (start us, length us, event | category | flops | bytes accessed | tf_op | source)
XLA Modules:
  0.0 89.0 jit_solution(13381750622013706368)
XLA Ops:
  0.7 1.1 %copy.11 = bf16[1,512,137]{2,1,0:T(8,128)(2,1)S(1)} copy(bf16[1,512,137]{1,2,0:T(8,128)(2,1)} %param.25) | data formatting | bytes 280576 | tf_op args[0]
  1.8 3.0 %collective-permute-start.2 = (bf16[256,137]{1,0:T(8,128)(2,1)S(1)}, bf16[256,137]{1,0:T(8,128)(2,1)S(1)}, u32[]{:S(2)}, u32[]{:S(2)}) collective-permute-start(bf16[256,137]{1,0:T(8,128)(2,1)S(1)} %get-tuple-element.793), channel_id=1, source_target_pairs={{0,1},{1,2},{2,3},{3,4},{4,5},{5,6},{6,7},{7,0},{8,9},{9,10},{10,1... | collective-permute-start | bytes 210440 | tf_op jit(solution)/shard_map/ppermute | solution.py:16
  4.8 3.1 %collective-permute-start.3 = (bf16[256,137]{1,0:T(8,128)(2,1)S(1)}, bf16[256,137]{1,0:T(8,128)(2,1)S(1)}, u32[]{:S(2)}, u32[]{:S(2)}) collective-permute-start(bf16[256,137]{1,0:T(8,128)(2,1)S(1)} %get-tuple-element.794), channel_id=1, source_target_pairs={{1,0},{2,1},{3,2},{4,3},{5,4},{6,5},{7,6},{0,7},{9,8},{10,9},{11,1... | collective-permute-start | bytes 210440 | tf_op jit(solution)/shard_map/ppermute | solution.py:18
  8.6 1.0 %slice_convert_fusion.7 = (f32[512,1]{0,1:T(1,128)S(1)}, f32[512,1]{0,1:T(1,128)S(1)}, f32[512,1]{0,1:T(1,128)S(1)}, f32[512,1]{0,1:T(1,128)S(1)}, f32[512,1]{0,...) fusion(bf16[512,8]{0,1:T(8,128)(2,1)} %param.27), kind=kLoop, calls=%fused_computation.82 | loop fusion | flops 4096 | bytes 24576 | tf_op jit(solution)/shard_map/jit(_where)/broadcast_in_dim | solution.py:38
  9.7 1.9 %add_convert_fusion.2 = bf16[512,1024]{1,0:T(8,128)(2,1)S(1)} fusion(f32[512]{0:T(512)S(1)} %bitcast.40, f32[512]{0:T(512)S(1)} %bitcast.42, f32[512]{0:T(512)S(1)} %bitcast.30, f32[512]{0:T(512)S(1)} %bitcast.32, f32[512]{0:T(512)S(1)} %bitcast.34, f32[512]{0:T(512)S(1)} %bitcast.36, f32[512]{0:T(512)S(1)} %bitcast.38, f32[512]{0:T(512)S(1)} %bitcast.28, ...), kind=kLoop, calls=%fused_computation.48 | loop fusion | flops 13107200 | bytes 1067008 | tf_op jit(solution)/shard_map/convert_element_type | solution.py:41
  11.6 1.0 %collective-permute-done.3 = bf16[256,137]{1,0:T(8,128)(2,1)S(1)} collective-permute-done((bf16[256,137]{1,0:T(8,128)(2,1)S(1)}, bf16[256,137]{1,0:T(8,128)(2,1)S(1)}, u32[]{:S(2)}, u32[]{:S(2)}) %collective-permute-start.3) | collective-permute-done | bytes 70176 | tf_op jit(solution)/shard_map/ppermute | solution.py:18
  12.6 0.1 pad_maximum_fusion
  12.7 1.2 %while.115 = (s32[]{:T(128)}, f32[512,137]{0,1:T(8,128)S(1)}, s32[]{:T(128)}, f32[512]{0:T(512)S(1)}, bf16[512,1024]{1,0:T(8,128)(2,1)S(1)}, /*index=5*/bf16[102...) while((s32[]{:T(128)}, f32[512,137]{0,1:T(8,128)S(1)}, s32[]{:T(128)}, ...), condition=%wide.region_1.2_spmd, body=%wide.region_0.1_spmd.sunk | while | flops 35948804 | bytes 936599 | solution.py:58
  12.8 0.3 fusion.63
  13.2 0.3 fusion.63
  13.6 0.3 fusion.63
  13.9 1.0 %copy-done.1 = bf16[512,1024]{1,0:T(8,128)(2,1)} copy-done((bf16[512,1024]{1,0:T(8,128)(2,1)}, bf16[512,1024]{1,0:T(8,128)(2,1)S(1)}, u32[]{:S(2)}) %copy-start.1) | copy-done | bytes 1048600
  14.9 29.6 %while.118 = (s32[]{:T(128)}, bf16[1024,137]{1,0:T(8,128)(2,1)S(1)}, f32[512,137]{0,1:T(8,128)S(1)}, s32[]{:T(128)}, s32[512]{0:T(512)S(1)}, /*index=5*/f32[512]...) while((s32[]{:T(128)}, bf16[1024,137]{1,0:T(8,128)(2,1)S(1)}, ...), condition=%wide.region_5.6_spmd.clone, body=%wide.region_2.5_spmd.clone.sunk | while | flops 49059600 | bytes 3693673 | solution.py:113
  14.9 1.8 %add_convert_fusion.5 = bf16[512,1024]{1,0:T(8,128)(2,1)S(1)} fusion(f32[512]{0:T(512)S(1)} %get-tuple-element.1334, f32[512]{0:T(512)S(1)} %get-tuple-element.1332, f32[512]{0:T(512)S(1)} %get-tuple-element.1331, f32[512]{0:T(512)S(1)} %get-tuple-element.1330, f32[512]{0:T(512)S(1)} %get-tuple-element.1329, f32[512]{0:T(512)S(1)} %get-tuple-element.1328, ...), kind=kLoop, calls=%fused_computation.24.clone.1 | loop fusion | flops 13107200 | bytes 1067008 | tf_op jit(solution)/shard_map/convert_element_type | solution.py:41
  16.8 6.7 %collective-permute-done.1 = bf16[1024,137]{1,0:T(8,128)(2,1)S(1)} collective-permute-done((bf16[1024,137]{1,0:T(8,128)(2,1)S(1)}, bf16[1024,137]{1,0:T(8,128)(2,1)S(1)}, u32[]{:S(2)}, u32[]{:S(2)}) %collective-permute-start.1) | collective-permute-done | bytes 280608 | tf_op jit(solution)/shard_map/while/body/eval_jaxpr/ppermute | solution.py:28
  23.5 1.2 %while.121 = (s32[]{:T(128)}, f32[512,137]{0,1:T(8,128)S(1)}, s32[]{:T(128)}, f32[512]{0:T(512)S(1)}, bf16[512,1024]{1,0:T(8,128)(2,1)S(1)}, /*index=5*/bf16[102...) while((s32[]{:T(128)}, f32[512,137]{0,1:T(8,128)S(1)}, s32[]{:T(128)}, ...), condition=%wide.region_4.4_spmd, body=%wide.region_3.3_spmd.sunk | while | flops 35948804 | bytes 936599 | solution.py:58
  23.6 0.3 fusion.68
  24.0 0.3 fusion.68
  24.4 0.3 fusion.68
  24.8 1.9 %add_convert_fusion.5 = bf16[512,1024]{1,0:T(8,128)(2,1)S(1)} fusion(f32[512]{0:T(512)S(1)} %get-tuple-element.1334, f32[512]{0:T(512)S(1)} %get-tuple-element.1332, f32[512]{0:T(512)S(1)} %get-tuple-element.1331, f32[512]{0:T(512)S(1)} %get-tuple-element.1330, f32[512]{0:T(512)S(1)} %get-tuple-element.1329, f32[512]{0:T(512)S(1)} %get-tuple-element.1328, ...), kind=kLoop, calls=%fused_computation.24.clone.1 | loop fusion | flops 13107200 | bytes 1067008 | tf_op jit(solution)/shard_map/convert_element_type | solution.py:41
  26.7 6.7 %collective-permute-done.1 = bf16[1024,137]{1,0:T(8,128)(2,1)S(1)} collective-permute-done((bf16[1024,137]{1,0:T(8,128)(2,1)S(1)}, bf16[1024,137]{1,0:T(8,128)(2,1)S(1)}, u32[]{:S(2)}, u32[]{:S(2)}) %collective-permute-start.1) | collective-permute-done | bytes 280608 | tf_op jit(solution)/shard_map/while/body/eval_jaxpr/ppermute | solution.py:28
  33.4 1.2 %while.121 = (s32[]{:T(128)}, f32[512,137]{0,1:T(8,128)S(1)}, s32[]{:T(128)}, f32[512]{0:T(512)S(1)}, bf16[512,1024]{1,0:T(8,128)(2,1)S(1)}, /*index=5*/bf16[102...) while((s32[]{:T(128)}, f32[512,137]{0,1:T(8,128)S(1)}, s32[]{:T(128)}, ...), condition=%wide.region_4.4_spmd, body=%wide.region_3.3_spmd.sunk | while | flops 35948804 | bytes 936599 | solution.py:58
  33.5 0.3 fusion.68
  33.9 0.3 fusion.68
  34.3 0.3 fusion.68
  34.7 1.9 %add_convert_fusion.5 = bf16[512,1024]{1,0:T(8,128)(2,1)S(1)} fusion(f32[512]{0:T(512)S(1)} %get-tuple-element.1334, f32[512]{0:T(512)S(1)} %get-tuple-element.1332, f32[512]{0:T(512)S(1)} %get-tuple-element.1331, f32[512]{0:T(512)S(1)} %get-tuple-element.1330, f32[512]{0:T(512)S(1)} %get-tuple-element.1329, f32[512]{0:T(512)S(1)} %get-tuple-element.1328, ...), kind=kLoop, calls=%fused_computation.24.clone.1 | loop fusion | flops 13107200 | bytes 1067008 | tf_op jit(solution)/shard_map/convert_element_type | solution.py:41
  36.6 6.7 %collective-permute-done.1 = bf16[1024,137]{1,0:T(8,128)(2,1)S(1)} collective-permute-done((bf16[1024,137]{1,0:T(8,128)(2,1)S(1)}, bf16[1024,137]{1,0:T(8,128)(2,1)S(1)}, u32[]{:S(2)}, u32[]{:S(2)}) %collective-permute-start.1) | collective-permute-done | bytes 280608 | tf_op jit(solution)/shard_map/while/body/eval_jaxpr/ppermute | solution.py:28
  43.3 1.2 %while.121 = (s32[]{:T(128)}, f32[512,137]{0,1:T(8,128)S(1)}, s32[]{:T(128)}, f32[512]{0:T(512)S(1)}, bf16[512,1024]{1,0:T(8,128)(2,1)S(1)}, /*index=5*/bf16[102...) while((s32[]{:T(128)}, f32[512,137]{0,1:T(8,128)S(1)}, s32[]{:T(128)}, ...), condition=%wide.region_4.4_spmd, body=%wide.region_3.3_spmd.sunk | while | flops 35948804 | bytes 936599 | solution.py:58
  43.4 0.3 fusion.68
  43.8 0.3 fusion.68
  44.2 0.3 fusion.68
  44.6 0.3 fusion.44
  44.9 0.2 convolution_convert_fusion
  45.1 0.1 copy.14
  45.3 0.3 copy-done.2
  45.6 4.2 %while.116 = (s32[]{:T(128)}, f32[1024,137]{0,1:T(8,128)S(1)}, s32[]{:T(128)}, bf16[512,1024]{1,0:T(8,128)(2,1)}, f32[512]{0:T(512)S(1)}, /*index=5*/bf16[512,13...) while((s32[]{:T(128)}, f32[1024,137]{0,1:T(8,128)S(1)}, s32[]{:T(128)}, ...), condition=%wide.region_7.8_spmd, body=%wide.region_6.7_spmd.sunk | while | flops 36106628 | bytes 1481367 | solution.py:73
  45.7 1.3 %convolution_add_fusion.4 = f32[1024,137]{0,1:T(8,128)S(1)} fusion(f32[1024,137]{0,1:T(8,128)S(1)} %get-tuple-element.1354, bf16[512,1024]{1,0:T(8,128)(2,1)} %get-tuple-element.1366, s32[]{:T(128)S(6)} %select_n.307, bf16[512,137]{1,0:T(8,128)(2,1)S(1)} %get-tuple-element.1368, f32[128]{0:T(128)S(1)} %dynamic_slice.71), kind=kOutput, calls=%fused_computation.12.clone.1 | convolution fusion | flops 36106624 | bytes 1480192 | tf_op jit(solution)/shard_map/while/body/dot_general | solution.py:69
  47.1 1.3 %convolution_add_fusion.4 = f32[1024,137]{0,1:T(8,128)S(1)} fusion(f32[1024,137]{0,1:T(8,128)S(1)} %get-tuple-element.1354, bf16[512,1024]{1,0:T(8,128)(2,1)} %get-tuple-element.1366, s32[]{:T(128)S(6)} %select_n.307, bf16[512,137]{1,0:T(8,128)(2,1)S(1)} %get-tuple-element.1368, f32[128]{0:T(128)S(1)} %dynamic_slice.71), kind=kOutput, calls=%fused_computation.12.clone.1 | convolution fusion | flops 36106624 | bytes 1480192 | tf_op jit(solution)/shard_map/while/body/dot_general | solution.py:69
  48.5 1.3 %convolution_add_fusion.4 = f32[1024,137]{0,1:T(8,128)S(1)} fusion(f32[1024,137]{0,1:T(8,128)S(1)} %get-tuple-element.1354, bf16[512,1024]{1,0:T(8,128)(2,1)} %get-tuple-element.1366, s32[]{:T(128)S(6)} %select_n.307, bf16[512,137]{1,0:T(8,128)(2,1)S(1)} %get-tuple-element.1368, f32[128]{0:T(128)S(1)} %dynamic_slice.71), kind=kOutput, calls=%fused_computation.12.clone.1 | convolution fusion | flops 36106624 | bytes 1480192 | tf_op jit(solution)/shard_map/while/body/dot_general | solution.py:69
  49.8 28.4 %while.120 = (s32[]{:T(128)}, f32[1024,137]{0,1:T(8,128)S(1)}, s32[]{:T(128)}, s32[512]{0:T(512)S(1)}, f32[512]{0:T(512)S(1)}, /*index=5*/s32[]{:T(128)}, bf16[5...) while((s32[]{:T(128)}, f32[1024,137]{0,1:T(8,128)S(1)}, ...), condition=%wide.region_11.12_spmd.clone, body=%wide.region_8.11_spmd.clone.sunk | while | flops 49357712 | bytes 7044213 | solution.py:125
  49.9 1.9 %add_convert_fusion.6 = bf16[512,1024]{1,0:T(8,128)(2,1)S(1)} fusion(f32[512]{0:T(512)S(1)} %get-tuple-element.1438, f32[512]{0:T(512)S(1)} %get-tuple-element.1436, f32[512]{0:T(512)S(1)} %get-tuple-element.1435, f32[512]{0:T(512)S(1)} %get-tuple-element.1434, f32[512]{0:T(512)S(1)} %get-tuple-element.1433, f32[512]{0:T(512)S(1)} %get-tuple-element.1432, ...), kind=kLoop, calls=%fused_computation.36.clone.1 | loop fusion | flops 13107200 | bytes 1067008 | tf_op jit(solution)/shard_map/convert_element_type | solution.py:41
  51.9 1.4 %while.122 = (s32[]{:T(128)}, f32[1024,137]{0,1:T(8,128)S(1)}, s32[]{:T(128)}, bf16[512,1024]{1,0:T(8,128)(2,1)S(1)}, f32[512]{0:T(512)S(1)}, /*index=5*/bf16[51...) while((s32[]{:T(128)}, f32[1024,137]{0,1:T(8,128)S(1)}, s32[]{:T(128)}, ...), condition=%wide.region_10.10_spmd, body=%wide.region_9.9_spmd.sunk | while | flops 36106628 | bytes 1481367 | solution.py:73
  51.9 0.1 dynamic_slice.74
  52.0 0.4 convolution_add_fusion.5
  52.4 0.4 convolution_add_fusion.5
  52.9 0.4 convolution_add_fusion.5
  53.3 5.9 %collective-permute-done = f32[1024,137]{0,1:T(8,128)S(1)} collective-permute-done((f32[1024,137]{0,1:T(8,128)S(1)}, f32[1024,137]{0,1:T(8,128)S(1)}, u32[]{:S(2)}, u32[]{:S(2)}) %collective-permute-start) | collective-permute-done | bytes 561184 | tf_op jit(solution)/shard_map/while/body/eval_jaxpr/ppermute | solution.py:28
  59.4 1.9 %add_convert_fusion.6 = bf16[512,1024]{1,0:T(8,128)(2,1)S(1)} fusion(f32[512]{0:T(512)S(1)} %get-tuple-element.1438, f32[512]{0:T(512)S(1)} %get-tuple-element.1436, f32[512]{0:T(512)S(1)} %get-tuple-element.1435, f32[512]{0:T(512)S(1)} %get-tuple-element.1434, f32[512]{0:T(512)S(1)} %get-tuple-element.1433, f32[512]{0:T(512)S(1)} %get-tuple-element.1432, ...), kind=kLoop, calls=%fused_computation.36.clone.1 | loop fusion | flops 13107200 | bytes 1067008 | tf_op jit(solution)/shard_map/convert_element_type | solution.py:41
  61.3 1.4 %while.122 = (s32[]{:T(128)}, f32[1024,137]{0,1:T(8,128)S(1)}, s32[]{:T(128)}, bf16[512,1024]{1,0:T(8,128)(2,1)S(1)}, f32[512]{0:T(512)S(1)}, /*index=5*/bf16[51...) while((s32[]{:T(128)}, f32[1024,137]{0,1:T(8,128)S(1)}, s32[]{:T(128)}, ...), condition=%wide.region_10.10_spmd, body=%wide.region_9.9_spmd.sunk | while | flops 36106628 | bytes 1481367 | solution.py:73
  61.4 0.4 convolution_add_fusion.5
  61.9 0.4 convolution_add_fusion.5
  62.4 0.4 convolution_add_fusion.5
  62.8 5.9 %collective-permute-done = f32[1024,137]{0,1:T(8,128)S(1)} collective-permute-done((f32[1024,137]{0,1:T(8,128)S(1)}, f32[1024,137]{0,1:T(8,128)S(1)}, u32[]{:S(2)}, u32[]{:S(2)}) %collective-permute-start) | collective-permute-done | bytes 561184 | tf_op jit(solution)/shard_map/while/body/eval_jaxpr/ppermute | solution.py:28
  68.8 1.9 %add_convert_fusion.6 = bf16[512,1024]{1,0:T(8,128)(2,1)S(1)} fusion(f32[512]{0:T(512)S(1)} %get-tuple-element.1438, f32[512]{0:T(512)S(1)} %get-tuple-element.1436, f32[512]{0:T(512)S(1)} %get-tuple-element.1435, f32[512]{0:T(512)S(1)} %get-tuple-element.1434, f32[512]{0:T(512)S(1)} %get-tuple-element.1433, f32[512]{0:T(512)S(1)} %get-tuple-element.1432, ...), kind=kLoop, calls=%fused_computation.36.clone.1 | loop fusion | flops 13107200 | bytes 1067008 | tf_op jit(solution)/shard_map/convert_element_type | solution.py:41
  70.8 1.4 %while.122 = (s32[]{:T(128)}, f32[1024,137]{0,1:T(8,128)S(1)}, s32[]{:T(128)}, bf16[512,1024]{1,0:T(8,128)(2,1)S(1)}, f32[512]{0:T(512)S(1)}, /*index=5*/bf16[51...) while((s32[]{:T(128)}, f32[1024,137]{0,1:T(8,128)S(1)}, s32[]{:T(128)}, ...), condition=%wide.region_10.10_spmd, body=%wide.region_9.9_spmd.sunk | while | flops 36106628 | bytes 1481367 | solution.py:73
  70.9 0.4 convolution_add_fusion.5
  71.3 0.4 convolution_add_fusion.5
  71.8 0.4 convolution_add_fusion.5
  72.2 5.9 %collective-permute-done = f32[1024,137]{0,1:T(8,128)S(1)} collective-permute-done((f32[1024,137]{0,1:T(8,128)S(1)}, f32[1024,137]{0,1:T(8,128)S(1)}, u32[]{:S(2)}, u32[]{:S(2)}) %collective-permute-start) | collective-permute-done | bytes 561184 | tf_op jit(solution)/shard_map/while/body/eval_jaxpr/ppermute | solution.py:28
  78.3 6.4 %collective-permute-start.5 = (f32[256,137]{0,1:T(8,128)S(1)}, f32[256,137]{0,1:T(8,128)S(1)}, u32[]{:S(2)}, u32[]{:S(2)}) collective-permute-start(f32[256,137]{0,1:T(8,128)S(1)} %get-tuple-element.791), channel_id=1, source_target_pairs={{1,0},{2,1},{3,2},{4,3},{5,4},{6,5},{7,6},{0,7},{9,8},{10,9},{11,1... | collective-permute-start | bytes 420872 | tf_op jit(solution)/shard_map/ppermute | solution.py:28
  84.7 3.1 %collective-permute-done.4 = f32[256,137]{0,1:T(8,128)S(1)} collective-permute-done((f32[256,137]{0,1:T(8,128)S(1)}, f32[256,137]{0,1:T(8,128)S(1)}, u32[]{:S(2)}, u32[]{:S(2)}) %collective-permute-start.4) | collective-permute-done | bytes 140320 | tf_op jit(solution)/shard_map/ppermute | solution.py:28
  87.8 0.3 copy.16
  88.1 0.1 reshape_dynamic-update-slice_fusion
  88.3 0.7 copy-done.3
  (72 shorter events, 2.9 us)
Async XLA Ops:
  0.6 43.9 %copy-start = (bf16[137,128]{1,0:T(8,128)(2,1)S(1)}, bf16[137,128]{1,0:T(8,128)(2,1)}, u32[]{:S(2)}) copy-start(bf16[137,128]{1,0:T(8,128)(2,1)} %param.32) | copy-start | bytes 105220
  0.6 9.0 %copy-start.7 = (s32[512]{0:T(512)S(1)}, s32[512]{0:T(512)}, u32[]{:S(2)}) copy-start(s32[512]{0:T(512)} %param.26) | copy-start | bytes 6148
  0.7 9.0 %copy-start.6 = (s32[512]{0:T(512)S(1)}, s32[512]{0:T(512)}, u32[]{:S(2)}) copy-start(s32[512]{0:T(512)} %param.28) | copy-start | bytes 6148
  0.7 9.0 %copy-start.5 = (f32[512]{0:T(512)S(1)}, f32[512]{0:T(512)}, u32[]{:S(2)}) copy-start(f32[512]{0:T(512)} %param.29) | copy-start | bytes 6148
  1.8 9.8 %collective-permute-start.2 = (bf16[256,137]{1,0:T(8,128)(2,1)S(1)}, bf16[256,137]{1,0:T(8,128)(2,1)S(1)}, u32[]{:S(2)}, u32[]{:S(2)}) collective-permute-start(bf16[256,137]{1,0:T(8,128)(2,1)S(1)} %get-tuple-element.793), channel_id=1, source_target_pairs={{0,1},{1,2},{2,3},{3,4},{4,5},{5,6},{6,7},{7,0},{8,9},{9,10},{10,1... | collective-permute-start | bytes 210440 | tf_op jit(solution)/shard_map/ppermute | solution.py:16
  4.8 7.8 %collective-permute-start.3 = (bf16[256,137]{1,0:T(8,128)(2,1)S(1)}, bf16[256,137]{1,0:T(8,128)(2,1)S(1)}, u32[]{:S(2)}, u32[]{:S(2)}) collective-permute-start(bf16[256,137]{1,0:T(8,128)(2,1)S(1)} %get-tuple-element.794), channel_id=1, source_target_pairs={{1,0},{2,1},{3,2},{4,3},{5,4},{6,5},{7,6},{0,7},{9,8},{10,9},{11,1... | collective-permute-start | bytes 210440 | tf_op jit(solution)/shard_map/ppermute | solution.py:18
  13.9 1.0 %copy-start.1 = (bf16[512,1024]{1,0:T(8,128)(2,1)}, bf16[512,1024]{1,0:T(8,128)(2,1)S(1)}, u32[]{:S(2)}) copy-start(bf16[512,1024]{1,0:T(8,128)(2,1)S(1)} %get-tuple-element.1456) | copy-start | bytes 3145732
  13.9 30.7 %copy-start.4 = (f32[512,128]{1,0:T(8,128)S(1)}, f32[512,128]{1,0:T(8,128)}, u32[]{:S(2)}) copy-start(f32[512,128]{1,0:T(8,128)} %param.31) | copy-start | bytes 786436
  13.9 30.9 %copy-start.8 = (f32[128]{0:T(128)S(1)}, f32[128]{0:T(128)}, u32[]{:S(2)}) copy-start(f32[128]{0:T(128)} %param.33) | copy-start | bytes 1540
  14.9 8.6 %collective-permute-start.1 = (bf16[1024,137]{1,0:T(8,128)(2,1)S(1)}, bf16[1024,137]{1,0:T(8,128)(2,1)S(1)}, u32[]{:S(2)}, u32[]{:S(2)}) collective-permute-start(bf16[1024,137]{1,0:T(8,128)(2,1)S(1)} %get-tuple-element.1296), channel_id=1, source_target_pairs={{24,0},{0,8},{8,16},{16,24},{25,1},{1,9},{9,17},{17,25},{26,2},{2,... | collective-permute-start | bytes 841736 | tf_op jit(solution)/shard_map/while/body/eval_jaxpr/ppermute | solution.py:28
  24.8 8.7 %collective-permute-start.1 = (bf16[1024,137]{1,0:T(8,128)(2,1)S(1)}, bf16[1024,137]{1,0:T(8,128)(2,1)S(1)}, u32[]{:S(2)}, u32[]{:S(2)}) collective-permute-start(bf16[1024,137]{1,0:T(8,128)(2,1)S(1)} %get-tuple-element.1296), channel_id=1, source_target_pairs={{24,0},{0,8},{8,16},{16,24},{25,1},{1,9},{9,17},{17,25},{26,2},{2,... | collective-permute-start | bytes 841736 | tf_op jit(solution)/shard_map/while/body/eval_jaxpr/ppermute | solution.py:28
  34.7 8.7 %collective-permute-start.1 = (bf16[1024,137]{1,0:T(8,128)(2,1)S(1)}, bf16[1024,137]{1,0:T(8,128)(2,1)S(1)}, u32[]{:S(2)}, u32[]{:S(2)}) collective-permute-start(bf16[1024,137]{1,0:T(8,128)(2,1)S(1)} %get-tuple-element.1296), channel_id=1, source_target_pairs={{24,0},{0,8},{8,16},{16,24},{25,1},{1,9},{9,17},{17,25},{26,2},{2,... | collective-permute-start | bytes 841736 | tf_op jit(solution)/shard_map/while/body/eval_jaxpr/ppermute | solution.py:28
  44.9 0.7 copy-start.2
  49.8 9.4 %collective-permute-start = (f32[1024,137]{0,1:T(8,128)S(1)}, f32[1024,137]{0,1:T(8,128)S(1)}, u32[]{:S(2)}, u32[]{:S(2)}) collective-permute-start(f32[1024,137]{0,1:T(8,128)S(1)} %get-tuple-element.1399), channel_id=1, source_target_pairs={{24,0},{0,8},{8,16},{16,24},{25,1},{1,9},{9,17},{17,25},{26,2},{2,... | collective-permute-start | bytes 1683464 | tf_op jit(solution)/shard_map/while/body/eval_jaxpr/ppermute | solution.py:28
  59.3 9.4 %collective-permute-start = (f32[1024,137]{0,1:T(8,128)S(1)}, f32[1024,137]{0,1:T(8,128)S(1)}, u32[]{:S(2)}, u32[]{:S(2)}) collective-permute-start(f32[1024,137]{0,1:T(8,128)S(1)} %get-tuple-element.1399), channel_id=1, source_target_pairs={{24,0},{0,8},{8,16},{16,24},{25,1},{1,9},{9,17},{17,25},{26,2},{2,... | collective-permute-start | bytes 1683464 | tf_op jit(solution)/shard_map/while/body/eval_jaxpr/ppermute | solution.py:28
  68.7 9.4 %collective-permute-start = (f32[1024,137]{0,1:T(8,128)S(1)}, f32[1024,137]{0,1:T(8,128)S(1)}, u32[]{:S(2)}, u32[]{:S(2)}) collective-permute-start(f32[1024,137]{0,1:T(8,128)S(1)} %get-tuple-element.1399), channel_id=1, source_target_pairs={{24,0},{0,8},{8,16},{16,24},{25,1},{1,9},{9,17},{17,25},{26,2},{2,... | collective-permute-start | bytes 1683464 | tf_op jit(solution)/shard_map/while/body/eval_jaxpr/ppermute | solution.py:28
  78.2 9.6 %collective-permute-start.4 = (f32[256,137]{0,1:T(8,128)S(1)}, f32[256,137]{0,1:T(8,128)S(1)}, u32[]{:S(2)}, u32[]{:S(2)}) collective-permute-start(f32[256,137]{0,1:T(8,128)S(1)} %get-tuple-element.792), channel_id=1, source_target_pairs={{7,0},{0,1},{1,2},{2,3},{3,4},{4,5},{5,6},{6,7},{15,8},{8,9},{9,10... | collective-permute-start | bytes 420872 | tf_op jit(solution)/shard_map/ppermute | solution.py:28
  78.3 9.8 %collective-permute-start.5 = (f32[256,137]{0,1:T(8,128)S(1)}, f32[256,137]{0,1:T(8,128)S(1)}, u32[]{:S(2)}, u32[]{:S(2)}) collective-permute-start(f32[256,137]{0,1:T(8,128)S(1)} %get-tuple-element.791), channel_id=1, source_target_pairs={{1,0},{2,1},{3,2},{4,3},{5,4},{6,5},{7,6},{0,7},{9,8},{10,9},{11,1... | collective-permute-start | bytes 420872 | tf_op jit(solution)/shard_map/ppermute | solution.py:28
  88.3 0.7 copy-start.3
where the time goes:
time: 90 us; the launch traced here: 89 us
  waiting for transfers between devices  41.9 us (47%)
  other arithmetic  14.4 us (16%)
  starting transfers between devices  12.9 us (14%)
  matrix products  11.2 us (12%)
  local copies, waits for them, and re-layouts  5.86 us (7%)
  between operations  1.64 us (2%)
  loops' own time  1.15 us (1%)
    ppermute x8, waiting for transfers between devices, shifted(): return lax.ppermute(block, axis, route)  40.9 us
    convert_element_type x7, other arithmetic, footprint_matrix(): return matrix.astype(jnp.bfloat16)  13 us
    dot_general x12, matrix products, spread_one_block(): lax.dot_general(rows, part, (((0,), (0,)), ((), ())), preferred_element_t...  7.2 us
    ppermute x8, starting transfers between devices, shifted(): return lax.ppermute(block, axis, route)  6.73 us
    dot_general x12, matrix products, gather_one_block(): part = jnp.dot(rows, wide, preferred_element_type=jnp.float32)  3.52 us
    ppermute x1, starting transfers between devices, with_halo(): lax.ppermute(head, axis, [((i + 1) % count, i) for i in range(count)])  3.1 us
    unnamed x19, local copies, waits for them, and re-layouts  3.06 us
    ppermute x1, starting transfers between devices, with_halo(): lax.ppermute(tail, axis, [(i, (i + 1) % count) for i in range(count)])  3.02 us
  transfers between devices with their start and end apart: 10, of which 8 were waited for; matrix products, arithmetic and copies ran while one was open for 21% of the time, Pallas kernels for 0%

commit v1 on v0

v1 whole, which is shorter than its diff:
```python
import functools

import jax
import jax.numpy as jnp
from jax import lax
from jax.experimental import pallas as pl
from jax.experimental.pallas import tpu as pltpu
from jax.sharding import PartitionSpec as P

MESH = pl.DeviceIdType.MESH
F32 = jnp.float32
BF16 = jnp.bfloat16
GROUP = 128
CORES = 2


def nt_dot(a, b):
    return lax.dot_general(a, b, (((1,), (1,)), ((), ())), preferred_element_type=F32)


def nn_dot(a, b):
    return jnp.dot(a, b, preferred_element_type=F32)


def message_names(n_tm, chunks):
    ny = n_tm // CORES
    names = [("meta_i", r) for r in range(1, n_tm)]
    names += [("meta_f", r) for r in range(1, n_tm)]
    names += [("halo", side) for side in range(2)]
    names += [("pair", dy, k) for dy in range(ny) for k in range(chunks)]
    names += [("sum", dy, k) for dy in range(1, ny) for k in range(chunks)]
    names += [("scaled", r, k) for r in range(1, n_tm) for k in range(chunks)]
    names += [("rim", side) for side in range(2)]
    return {name: index for index, name in enumerate(names)}


def kernel(
    n_tm,
    n_space,
    chunks,
    state_ref,
    start_ref,
    weight_ref,
    slot_ref,
    frac_ref,
    live_ref,
    values_ref,
    jac_ref,
    inv_ref,
    dep_ref,
    adj_ref,
    wide,
    meta_i,
    meta_f,
    foot_t,
    partial,
    values_t,
    inv_t,
    pair_out,
    pair_in,
    sum_out,
    sum_in,
    scaled,
    total,
    rim_out,
    rim_in,
    dep_t,
    send_sems,
    recv_sems,
):
    ny = n_tm // CORES
    turn = lax.axis_index("tm")
    tile = lax.axis_index("space")
    row = turn // CORES
    core = lax.rem(turn, CORES)
    left = lax.rem(tile + n_space - 1, n_space)
    right = lax.rem(tile + 1, n_space)
    levels, cols_dev = state_ref.shape
    halo_w = cols_dev // 2
    width = cols_dev + 2 * halo_w
    foot, obs = weight_ref.shape
    chunk_w = obs // chunks
    names = message_names(n_tm, chunks)

    def peer(r):
        dy, dc = r // CORES, r % CORES
        return (lax.rem(row + dy, ny) * CORES + lax.rem(core + dc, CORES), tile)

    def inverse(r):
        return ((ny - r // CORES) % ny) * CORES + r % CORES

    barrier = pltpu.get_barrier_semaphore()
    targets = [(turn, left), (turn, right)] + [peer(r) for r in range(1, n_tm)]
    for target in targets:
        pl.semaphore_signal(barrier, inc=1, device_id=target, device_id_type=MESH)

    started = []

    def send(name, name_there, src, dst, device):
        copy = pltpu.make_async_remote_copy(
            src_ref=src,
            dst_ref=dst,
            send_sem=send_sems.at[names[name]],
            recv_sem=recv_sems.at[names[name_there]],
            device_id=device,
            device_id_type=MESH,
        )
        copy.start()
        started.append(copy)

    def arrived(name, dst, device):
        pltpu.make_async_remote_copy(
            src_ref=dst,
            dst_ref=dst,
            send_sem=send_sems.at[names[name]],
            recv_sem=recv_sems.at[names[name]],
            device_id=device,
            device_id_type=MESH,
        ).wait_recv()

    jac = jac_ref[...]
    chan = jac.shape[1]
    eye = (
        lax.broadcasted_iota(jnp.int32, (chan, chan), 0)
        == lax.broadcasted_iota(jnp.int32, (chan, chan), 1)
    ).astype(F32).astype(BF16)
    jac_t = nt_dot(eye, jac).astype(BF16)
    own = nn_dot(jac_t, state_ref[...]).astype(BF16)
    wide[1] = own[:, :halo_w]
    wide[2] = own[:, halo_w:]

    total_cols = cols_dev * n_space
    local = start_ref[...] - tile * cols_dev + halo_w
    local = jnp.where(local < 0, local + total_cols, local)
    local = jnp.where(local >= total_cols, local - total_cols, local)
    meta_i[0, 0:1] = local
    meta_i[0, 1:2] = slot_ref[...]
    frac = frac_ref[...]
    weight = weight_ref[...].astype(F32)
    meta_f[0] = jnp.concatenate([weight * (1.0 - frac), weight * frac], axis=0).astype(BF16)

    pl.semaphore_wait(barrier, len(targets))
    send(("halo", 0), ("halo", 1), wide.at[1], wide.at[3], (turn, left))
    send(("halo", 1), ("halo", 0), wide.at[2], wide.at[0], (turn, right))
    for r in range(1, n_tm):
        back = inverse(r)
        send(("meta_i", r), ("meta_i", back), meta_i.at[0], meta_i.at[back], peer(r))
        send(("meta_f", r), ("meta_f", back), meta_f.at[0], meta_f.at[back], peer(r))

    def build(r):
        start = meta_i[r, 0:1]
        slot = meta_i[r, 1:2]
        pairs = meta_f[r].astype(F32)
        weights = jnp.where(slot == turn, pairs[:foot], 0.0)
        weights = weights + jnp.where(slot + 1 == turn, pairs[foot:], 0.0)
        place = lax.broadcasted_iota(jnp.int32, (GROUP, obs), 0)
        offset = jnp.bitwise_and(place - start, GROUP - 1)
        group = jnp.right_shift(start + offset, 7)
        value = jnp.zeros((GROUP, obs), F32)
        for k in range(foot):
            value = jnp.where(offset == k, weights[k : k + 1], value)
        for j in range(width // GROUP):
            block = jnp.where(group == j, value, 0.0).astype(BF16)
            foot_t[r, j * GROUP : (j + 1) * GROUP, :] = block

    def project(r, b):
        return nn_dot(wide[b], foot_t[r, b * halo_w : (b + 1) * halo_w, :])

    build(0)
    partial[0] = project(0, 1) + project(0, 2)
    values_t[...] = values_ref[...].T
    inv_t[...] = jnp.broadcast_to(inv_ref[...], (GROUP, chan)).T
    order = [r for r in range(1, n_tm)]
    for r in order:
        arrived(("meta_i", r), meta_i.at[r], peer(r))
        arrived(("meta_f", r), meta_f.at[r], peer(r))
        build(r)
        partial[r] = project(r, 1) + project(r, 2)

    arrived(("halo", 0), wide.at[0], (turn, left))
    arrived(("halo", 1), wide.at[3], (turn, right))

    def finish(r, k):
        lanes = slice(k * chunk_w, (k + 1) * chunk_w)
        edge = nn_dot(wide[0], foot_t[r, 0:halo_w, lanes])
        edge = edge + nn_dot(wide[3], foot_t[r, width - halo_w :, lanes])
        return partial[r, :, lanes] + edge

    for dy in range(1, ny):
        for k in range(chunks):
            pair_out[dy, k] = finish(dy * CORES + 1, k).astype(BF16)
            send(("pair", dy, k), ("pair", dy, k), pair_out.at[dy, k], pair_in.at[dy, k], peer(1))
    for dy in range(1, ny):
        back = ny - dy
        for k in range(chunks):
            mine = finish(dy * CORES, k)
            arrived(("pair", dy, k), pair_in.at[dy, k], peer(1))
            sum_out[dy, k] = (mine + pair_in[dy, k].astype(F32)).astype(BF16)
            send(("sum", dy, k), ("sum", back, k), sum_out.at[dy, k], sum_in.at[back, k], peer(dy * CORES))
    for k in range(chunks):
        pair_out[0, k] = finish(1, k).astype(BF16)
        send(("pair", 0, k), ("pair", 0, k), pair_out.at[0, k], pair_in.at[0, k], peer(1))
    for k in range(chunks):
        lanes = slice(k * chunk_w, (k + 1) * chunk_w)
        partial[0, :, lanes] = finish(0, k)
    for k in range(chunks):
        lanes = slice(k * chunk_w, (k + 1) * chunk_w)
        arrived(("pair", 0, k), pair_in.at[0, k], peer(1))
        projected = partial[0, :, lanes] + pair_in[0, k].astype(F32)
        for dy in range(1, ny):
            arrived(("sum", dy, k), sum_in.at[dy, k], peer(dy * CORES))
            projected = projected + sum_in[dy, k].astype(F32)
        place = lax.broadcasted_iota(jnp.int32, (chan, chunk_w), 1) + k * chunk_w
        departure = jnp.where(place < live_ref[0, 0], values_t[:, lanes] - projected, 0.0)
        dep_t[:, lanes] = departure
        scale = jnp.concatenate([inv_t[...]] * (chunk_w // GROUP), axis=1)
        scaled[0, k] = (departure * scale).astype(BF16)
        for dy in range(1, ny):
            r = dy * CORES
            back = inverse(r)
            send(("scaled", r, k), ("scaled", back, k), scaled.at[0, k], scaled.at[back, k], peer(r))
        send(("scaled", 1, k), ("scaled", 1, k), scaled.at[0, k], scaled.at[1, k], peer(1))

    def spread(r, k, b):
        lanes = slice(k * chunk_w, (k + 1) * chunk_w)
        return nt_dot(scaled[r, k], foot_t[r, b * halo_w : (b + 1) * halo_w, lanes])

    dep_ref[...] = dep_t[...].T
    for b in range(4):
        here = spread(0, 0, b)
        for k in range(1, chunks):
            here = here + spread(0, k, b)
        total[b] = here
    for k in range(chunks):
        arrived(("scaled", 1, k), scaled.at[1, k], peer(1))
    for b in range(4):
        here = total[b]
        for k in range(chunks):
            here = here + spread(1, k, b)
        total[b] = here
    for k in range(chunks):
        for dy in range(1, ny):
            r = dy * CORES
            arrived(("scaled", r, k), scaled.at[r, k], peer(r))
            send(("scaled", r + 1, k), ("scaled", r + 1, k), scaled.at[r, k], scaled.at[r + 1, k], peer(1))
        for dy in range(1, ny):
            for b in range(4):
                total[b] = total[b] + spread(dy * CORES, k, b)
    for dy in range(1, ny):
        for k in range(chunks):
            arrived(("scaled", dy * CORES + 1, k), scaled.at[dy * CORES + 1, k], peer(1))

    def last(b):
        here = total[b]
        for dy in range(1, ny):
            for k in range(chunks):
                here = here + spread(dy * CORES + 1, k, b)
        return here

    rim_out[0] = last(0).astype(BF16)
    send(("rim", 0), ("rim", 1), rim_out.at[0], rim_in.at[1], (turn, left))
    rim_out[1] = last(3).astype(BF16)
    send(("rim", 1), ("rim", 0), rim_out.at[1], rim_in.at[0], (turn, right))
    core_sums = [last(1), last(2)]
    for side in range(2):
        arrived(("rim", side), rim_in.at[side], (turn, (left, right)[side]))
        columns = (core_sums[side] + rim_in[side].astype(F32)).astype(BF16)
        adj_ref[:, side * halo_w : (side + 1) * halo_w] = nn_dot(jac, columns)
    for copy in started:
        copy.wait_send()


def body(
    state, obs_start, foot_weight, obs_slot, obs_frac, live_count, obs_values, jacobian, inv_var
):
    n_tm = lax.axis_size("tm")
    n_space = lax.axis_size("space")
    ny = n_tm // CORES
    chunks = 2
    _, cols_dev, levels = state.shape
    obs, chan = obs_values.shape
    foot = foot_weight.shape[1]
    halo_w = cols_dev // 2
    width = cols_dev + 2 * halo_w
    chunk_w = obs // chunks
    vmem = pl.BlockSpec(memory_space=pltpu.VMEM)
    smem = pl.BlockSpec(memory_space=pltpu.SMEM)
    count = len(message_names(n_tm, chunks))
    departures, adjoint_t = pl.pallas_call(
        functools.partial(kernel, n_tm, n_space, chunks),
        name="departures_and_adjoint",
        out_shape=(
            jax.ShapeDtypeStruct((obs, chan), F32),
            jax.ShapeDtypeStruct((levels, cols_dev), F32),
        ),
        in_specs=[vmem, vmem, vmem, vmem, vmem, smem, vmem, vmem, vmem],
        out_specs=(vmem, vmem),
        scratch_shapes=[
            pltpu.VMEM((4, chan, halo_w), BF16),
            pltpu.VMEM((n_tm, 2, obs), jnp.int32),
            pltpu.VMEM((n_tm, 2 * foot, obs), BF16),
            pltpu.VMEM((n_tm, width, obs), BF16),
            pltpu.VMEM((n_tm, chan, obs), F32),
            pltpu.VMEM((chan, obs), F32),
            pltpu.VMEM((chan, GROUP), F32),
            pltpu.VMEM((ny, chunks, chan, chunk_w), BF16),
            pltpu.VMEM((ny, chunks, chan, chunk_w), BF16),
            pltpu.VMEM((ny, chunks, chan, chunk_w), BF16),
            pltpu.VMEM((ny, chunks, chan, chunk_w), BF16),
            pltpu.VMEM((n_tm, chunks, chan, chunk_w), BF16),
            pltpu.VMEM((4, chan, halo_w), F32),
            pltpu.VMEM((2, chan, halo_w), BF16),
            pltpu.VMEM((2, chan, halo_w), BF16),
            pltpu.VMEM((chan, obs), F32),
            pltpu.SemaphoreType.DMA((count,)),
            pltpu.SemaphoreType.DMA((count,)),
        ],
        compiler_params=pltpu.CompilerParams(
            collective_id=0, has_side_effects=True, vmem_limit_bytes=48 * 1024 * 1024
        ),
    )(
        state[0].T,
        obs_start[None],
        foot_weight.T,
        obs_slot[None],
        obs_frac[None],
        live_count,
        obs_values,
        jacobian,
        inv_var[None],
    )
    return (departures, adjoint_t.T[None])


def solution(mesh):
    return jax.shard_map(
        body,
        mesh=mesh,
        in_specs=(
            P("tm", "space", None),
            P(("tm", "space")),
            P(("tm", "space"), None),
            P(("tm", "space")),
            P(("tm", "space")),
            P("tm", "space"),
            P(("tm", "space"), None),
            P(),
            P(),
        ),
        out_specs=(P(("tm", "space"), None), P("tm", "space", None)),
        check_vma=False,
    )
```

time: 90 us -> 34.6 us (0.38)
  waiting for transfers between devices: 41.9 us -> 0 us
  Pallas kernels: 0 us -> 27.3 us
  other arithmetic: 14.4 us -> 0 us
  starting transfers between devices: 12.9 us -> 0 us
  matrix products: 11.2 us -> 0 us
  loops' own time: 1.15 us -> 0 us
    ppermute x10 -> x0, waiting for transfers between devices: 41.9 us -> none  [the longest x8 40.9 us: shifted(): return lax.ppermute(block, axis, route)]
    pallas_call x0 -> x1, Pallas kernels: none -> 27.3 us  [body(): pl.pallas_call(functools.partial(kernel, n_tm, n_space, chunks), name='de...]
    convert_element_type x7 -> x0, other arithmetic: 13 us -> none  [footprint_matrix(): return matrix.astype(jnp.bfloat16)]
    ppermute x10 -> x0, starting transfers between devices: 12.9 us -> none  [the longest x8 6.73 us: shifted(): return lax.ppermute(block, axis, route)]
    dot_general x26 -> x0, matrix products: 11.2 us -> none  [the longest x12 7.2 us: spread_one_block(): lax.dot_general(rows, part, (((0,), (0,)), ((), ())), preferred_element_t...]
    unnamed x19 -> x18, local copies, waits for them, and re-layouts: 3.06 us -> 5.68 us
    dynamic_slice x24 -> x0, local copies, waits for them, and re-layouts: 1.83 us -> none  [the longest x12 0.92 us: spread_one_block(): scale = lax.dynamic_slice_in_dim(weight, first, block_rows, 0)]
    another operation x10 -> x0, loops' own time: 1.15 us -> none  [the longest x4 0.38 us: spread_slot(): lax.fori_loop(0, blocks, spread_one_block, jnp.zeros((width, levels), jnp...]
  transfers between devices with their start and end apart: 10 -> 0, of which waited for: 8 -> 0; matrix products, arithmetic and copies ran while one was open for 21% -> 0% of each run, Pallas kernels for 0% -> 0%
where the time goes in v1:
time: 34.6 us; the launch traced here: 34.3 us
  Pallas kernels  27.3 us (79%)
  local copies, waits for them, and re-layouts  5.68 us (16%)
  between operations  1.35 us (4%)
    pallas_call x1, Pallas kernels, body(): pl.pallas_call(functools.partial(kernel, n_tm, n_space, chunks), name='de...  27.3 us
    unnamed x18, local copies, waits for them, and re-layouts  5.68 us

profile of v1, /device:TPU:0, one launch (start us, length us, event | category | flops | bytes accessed | tf_op | source)
XLA Modules:
  0.0 34.3 jit_solution(17293694038936913378)
XLA Ops:
  0.6 0.0 copy-start.3
  1.3 0.0 copy-start.5
  1.3 0.0 copy-start.4
  1.3 0.0 copy-start.7
  1.3 0.0 copy-done.3
  1.3 0.6 %copy-done.5 = s32[512]{0:T(512)S(1)} copy-done((s32[512]{0:T(512)S(1)}, s32[512]{0:T(512)}, u32[]{:S(2)}) %copy-start.5) | copy-done | bytes 2072
  2.0 0.0 copy-done.4
  2.0 0.0 copy-done.7
  2.0 0.0 copy-start
  2.0 0.9 %copy-done = f32[512,128]{1,0:T(8,128)S(1)} copy-done((f32[512,128]{1,0:T(8,128)S(1)}, f32[512,128]{1,0:T(8,128)}, u32[]{:S(2)}) %copy-start) | copy-done | bytes 262168
  3.0 0.0 copy-start.1
  3.0 0.9 %copy-done.1 = bf16[1,512,137]{1,2,0:T(8,128)(2,1)S(1)} copy-done((bf16[1,512,137]{1,2,0:T(8,128)(2,1)S(1)}, bf16[1,512,137]{1,2,0:T(8,128)(2,1)}, u32[]{:S(2)}) %copy-start.1) | copy-done | bytes 140312
  3.9 0.0 copy-start.2
  3.9 0.8 %copy-done.2 = bf16[137,128]{1,0:T(8,128)(2,1)S(1)} copy-done((bf16[137,128]{1,0:T(8,128)(2,1)S(1)}, bf16[137,128]{1,0:T(8,128)(2,1)}, u32[]{:S(2)}) %copy-start.2) | copy-done | bytes 35096
  4.6 0.0 copy-start.6
  4.6 0.7 %copy-done.6 = f32[512]{0:T(512)S(1)} copy-done((f32[512]{0:T(512)S(1)}, f32[512]{0:T(512)}, u32[]{:S(2)}) %copy-start.6) | copy-done | bytes 2072
  5.3 27.3 %departures_and_adjoint.1 = (f32[512,128]{1,0:T(8,128)S(1)}, f32[137,512]{1,0:T(8,128)S(1)}) custom-call(bf16[137,512]{1,0:T(8,128)(2,1)S(1)} %bitcast.12, s32[1,512]{1,0:T(1,128)S(1)} %bitcast.14, bf16[8,512]{1,0:T(8,128)(2,1)S(1)} %bitcast.13, s32[1,512]{1,0:T(1,128)S(1)} %bitcast.15, f32[1,512]{1,0:T(1,128)S(1)} %bitcast.16, s32[1,1]{1,0:T(1,128)S(6)} %copy.13.live_ref, ...), custom_call_target="tpu_custom_call" | custom-call | tf_op jit(solution)/shard_map/departures_and_adjoint/pallas_call | solution.py:289
  32.6 1.0 %copy.11 = f32[1,512,137]{1,0,2:T(1,128)} copy(f32[1,512,137]{1,2,0:T(8,128)S(1)} %bitcast.11) | data formatting | bytes 561152
  33.6 0.7 %copy.14 = f32[512,128]{1,0:T(8,128)} copy(f32[512,128]{1,0:T(8,128)S(1)} %get-tuple-element.10) | data formatting | bytes 524288
Async XLA Ops:
  0.6 0.7 %copy-start.3 = (bf16[512,8]{0,1:T(8,128)(2,1)S(1)}, bf16[512,8]{0,1:T(8,128)(2,1)}, u32[]{:S(2)}) copy-start(bf16[512,8]{0,1:T(8,128)(2,1)} %param.11) | copy-start | bytes 24580
  1.3 0.7 %copy-start.5 = (s32[512]{0:T(512)S(1)}, s32[512]{0:T(512)}, u32[]{:S(2)}) copy-start(s32[512]{0:T(512)} %param.12) | copy-start | bytes 6148
  1.3 0.7 %copy-start.4 = (s32[512]{0:T(512)S(1)}, s32[512]{0:T(512)}, u32[]{:S(2)}) copy-start(s32[512]{0:T(512)} %param.10) | copy-start | bytes 6148
  1.3 0.7 %copy-start.7 = (f32[128]{0:T(128)S(1)}, f32[128]{0:T(128)}, u32[]{:S(2)}) copy-start(f32[128]{0:T(128)} %param.17) | copy-start | bytes 1540
  2.0 1.0 %copy-start = (f32[512,128]{1,0:T(8,128)S(1)}, f32[512,128]{1,0:T(8,128)}, u32[]{:S(2)}) copy-start(f32[512,128]{1,0:T(8,128)} %values_ref.1) | copy-start | bytes 786436
  3.0 0.9 %copy-start.1 = (bf16[1,512,137]{1,2,0:T(8,128)(2,1)S(1)}, bf16[1,512,137]{1,2,0:T(8,128)(2,1)}, u32[]{:S(2)}) copy-start(bf16[1,512,137]{1,2,0:T(8,128)(2,1)} %param.9) | copy-start | bytes 420868
  3.9 0.8 %copy-start.2 = (bf16[137,128]{1,0:T(8,128)(2,1)S(1)}, bf16[137,128]{1,0:T(8,128)(2,1)}, u32[]{:S(2)}) copy-start(bf16[137,128]{1,0:T(8,128)(2,1)} %jac_ref.1) | copy-start | bytes 105220
  4.6 0.7 %copy-start.6 = (f32[512]{0:T(512)S(1)}, f32[512]{0:T(512)}, u32[]{:S(2)}) copy-start(f32[512]{0:T(512)} %param.13) | copy-start | bytes 6148

commit v2 on v1

--- a/solution.py
+++ b/solution.py
@@ -38,17 +38,25 @@
     n_tm,
     n_space,
     chunks,
+    state_hbm,
+    start_hbm,
+    weight_hbm,
+    slot_hbm,
+    frac_hbm,
+    live_ref,
+    values_hbm,
+    jac_hbm,
+    inv_hbm,
+    dep_ref,
+    sum_ref,
     state_ref,
     start_ref,
     weight_ref,
     slot_ref,
     frac_ref,
-    live_ref,
     values_ref,
     jac_ref,
     inv_ref,
-    dep_ref,
-    adj_ref,
     wide,
     meta_i,
     meta_f,
@@ -65,6 +73,7 @@
     rim_out,
     rim_in,
     dep_t,
+    load_sems,
     send_sems,
     recv_sems,
 ):
@@ -94,14 +103,33 @@
     for target in targets:
         pl.semaphore_signal(barrier, inc=1, device_id=target, device_id_type=MESH)
 
+    pairs_in = [
+        (state_hbm, state_ref),
+        (jac_hbm, jac_ref),
+        (start_hbm, start_ref),
+        (slot_hbm, slot_ref),
+        (frac_hbm, frac_ref),
+        (weight_hbm, weight_ref),
+        (inv_hbm, inv_ref),
+        (values_hbm, values_ref),
+    ]
+    loads = [
+        pltpu.make_async_copy(src, dst, load_sems.at[i]) for i, (src, dst) in enumerate(pairs_in)
+    ]
+    for load in loads:
+        load.start()
+
     started = []
 
     def send(name, name_there, src, dst, device):
+        send_at(names[name], names[name_there], src, dst, device)
+
+    def send_at(index, index_there, src, dst, device):
         copy = pltpu.make_async_remote_copy(
             src_ref=src,
             dst_ref=dst,
-            send_sem=send_sems.at[names[name]],
-            recv_sem=recv_sems.at[names[name_there]],
+            send_sem=send_sems.at[index],
+            recv_sem=recv_sems.at[index_there],
             device_id=device,
             device_id_type=MESH,
         )
@@ -117,6 +145,33 @@
             device_id=device,
             device_id_type=MESH,
         ).wait_recv()
+
+    def send_sides(name, sources, targets_there, source_index, target_index):
+        odd = lax.rem(tile, 2)
+        for side in (odd, 1 - odd):
+            device = (turn, lax.rem(tile + n_space - 1 + 2 * side, n_space))
+            base = names[(name, 0)]
+            send_at(
+                base + side,
+                base + 1 - side,
+                sources.at[source_index(side)],
+                targets_there.at[target_index(side)],
+                device,
+            )
+
+    for load in loads[2:6]:
+        load.wait()
+    total_cols = cols_dev * n_space
+    local = start_ref[...] - tile * cols_dev + halo_w
+    local = jnp.where(local < 0, local + total_cols, local)
+    local = jnp.where(local >= total_cols, local - total_cols, local)
+    meta_i[0, 0:1] = local
+    meta_i[0, 1:2] = slot_ref[...]
+    frac = frac_ref[...]
+    weight = weight_ref[...].astype(F32)
+    meta_f[0] = jnp.concatenate([weight * (1.0 - frac), weight * frac], axis=0).astype(BF16)
+    for load in loads[:2]:
+        load.wait()
 
     jac = jac_ref[...]
     chan = jac.shape[1]
@@ -129,19 +184,8 @@
     wide[1] = own[:, :halo_w]
     wide[2] = own[:, halo_w:]
 
-    total_cols = cols_dev * n_space
-    local = start_ref[...] - tile * cols_dev + halo_w
-    local = jnp.where(local < 0, local + total_cols, local)
-    local = jnp.where(local >= total_cols, local - total_cols, local)
-    meta_i[0, 0:1] = local
-    meta_i[0, 1:2] = slot_ref[...]
-    frac = frac_ref[...]
-    weight = weight_ref[...].astype(F32)
-    meta_f[0] = jnp.concatenate([weight * (1.0 - frac), weight * frac], axis=0).astype(BF16)
-
     pl.semaphore_wait(barrier, len(targets))
-    send(("halo", 0), ("halo", 1), wide.at[1], wide.at[3], (turn, left))
-    send(("halo", 1), ("halo", 0), wide.at[2], wide.at[0], (turn, right))
+    send_sides("halo", wide, wide, lambda side: 1 + side, lambda side: 3 - 3 * side)
     for r in range(1, n_tm):
         back = inverse(r)
         send(("meta_i", r), ("meta_i", back), meta_i.at[0], meta_i.at[back], peer(r))
@@ -168,6 +212,8 @@
 
     build(0)
     partial[0] = project(0, 1) + project(0, 2)
+    for load in loads[6:]:
+        load.wait()
     values_t[...] = values_ref[...].T
     inv_t[...] = jnp.broadcast_to(inv_ref[...], (GROUP, chan)).T
     order = [r for r in range(1, n_tm)]
@@ -258,16 +304,29 @@
         return here
 
     rim_out[0] = last(0).astype(BF16)
-    send(("rim", 0), ("rim", 1), rim_out.at[0], rim_in.at[1], (turn, left))
     rim_out[1] = last(3).astype(BF16)
-    send(("rim", 1), ("rim", 0), rim_out.at[1], rim_in.at[0], (turn, right))
+    send_sides("rim", rim_out, rim_in, lambda side: side, lambda side: 1 - side)
     core_sums = [last(1), last(2)]
     for side in range(2):
         arrived(("rim", side), rim_in.at[side], (turn, (left, right)[side]))
-        columns = (core_sums[side] + rim_in[side].astype(F32)).astype(BF16)
-        adj_ref[:, side * halo_w : (side + 1) * halo_w] = nn_dot(jac, columns)
+        sum_ref[side] = (core_sums[side] + rim_in[side].astype(F32)).astype(BF16)
     for copy in started:
         copy.wait_send()
+
+
+def finish_kernel(dep_ref, sum_ref, jac_ref, dep_hbm, adj_hbm, adj_ref, sems):
+    dep_copy = pltpu.make_async_copy(dep_ref, dep_hbm, sems.at[0])
+    dep_copy.start()
+    jac = jac_ref[...]
+    levels = jac.shape[0]
+    halo_w = sum_ref.shape[2]
+    for side in range(2):
+        lanes = slice(side * halo_w, (side + 1) * halo_w)
+        adj_ref[:, :, lanes] = nn_dot(jac, sum_ref[side]).reshape(levels, 1, halo_w)
+    adj_copy = pltpu.make_async_copy(adj_ref, adj_hbm, sems.at[1])
+    adj_copy.start()
+    dep_copy.wait()
+    adj_copy.wait()
 
 
 def body(
@@ -276,7 +335,7 @@
     n_tm = lax.axis_size("tm")
     n_space = lax.axis_size("space")
     ny = n_tm // CORES
-    chunks = 2
+    chunks = 4
     _, cols_dev, levels = state.shape
     obs, chan = obs_values.shape
     foot = foot_weight.shape[1]
@@ -284,18 +343,27 @@
     width = cols_dev + 2 * halo_w
     chunk_w = obs // chunks
     vmem = pl.BlockSpec(memory_space=pltpu.VMEM)
-    smem = pl.BlockSpec(memory_space=pltpu.SMEM)
+    live_space = pl.BlockSpec(memory_space=pltpu.SMEM)
+    hbm = pl.BlockSpec(memory_space=pltpu.HBM)
     count = len(message_names(n_tm, chunks))
-    departures, adjoint_t = pl.pallas_call(
+    departures, sums = pl.pallas_call(
         functools.partial(kernel, n_tm, n_space, chunks),
         name="departures_and_adjoint",
         out_shape=(
-            jax.ShapeDtypeStruct((obs, chan), F32),
-            jax.ShapeDtypeStruct((levels, cols_dev), F32),
+            pltpu.VMEM((obs, chan), F32),
+            pltpu.VMEM((2, chan, halo_w), BF16),
         ),
-        in_specs=[vmem, vmem, vmem, vmem, vmem, smem, vmem, vmem, vmem],
+        in_specs=[hbm] * 5 + [live_space] + [hbm] * 3,
         out_specs=(vmem, vmem),
         scratch_shapes=[
+            pltpu.VMEM((levels, cols_dev), BF16),
+            pltpu.VMEM((1, obs), jnp.int32),
+            pltpu.VMEM((foot, obs), BF16),
+            pltpu.VMEM((1, obs), jnp.int32),
+            pltpu.VMEM((1, obs), F32),
+            pltpu.VMEM((obs, chan), F32),
+            pltpu.VMEM((levels, chan), BF16),
+            pltpu.VMEM((1, chan), F32),
             pltpu.VMEM((4, chan, halo_w), BF16),
             pltpu.VMEM((n_tm, 2, obs), jnp.int32),
             pltpu.VMEM((n_tm, 2 * foot, obs), BF16),
@@ -312,11 +380,12 @@
             pltpu.VMEM((2, chan, halo_w), BF16),
             pltpu.VMEM((2, chan, halo_w), BF16),
             pltpu.VMEM((chan, obs), F32),
+            pltpu.SemaphoreType.DMA((8,)),
             pltpu.SemaphoreType.DMA((count,)),
             pltpu.SemaphoreType.DMA((count,)),
         ],
         compiler_params=pltpu.CompilerParams(
-            collective_id=0, has_side_effects=True, vmem_limit_bytes=48 * 1024 * 1024
+            collective_id=0, has_side_effects=True, vmem_limit_bytes=58 * 1024 * 1024
         ),
     )(
         state[0].T,
@@ -329,7 +398,22 @@
         jacobian,
         inv_var[None],
     )
-    return (departures, adjoint_t.T[None])
+    departures, adjoint_t = pl.pallas_call(
+        finish_kernel,
+        name="write_outputs",
+        out_shape=(
+            jax.ShapeDtypeStruct((obs, chan), F32),
+            jax.ShapeDtypeStruct((levels, 1, cols_dev), F32),
+        ),
+        in_specs=[vmem, vmem, vmem],
+        out_specs=(hbm, hbm),
+        scratch_shapes=[
+            pltpu.VMEM((levels, 1, cols_dev), F32),
+            pltpu.SemaphoreType.DMA((2,)),
+        ],
+        compiler_params=pltpu.CompilerParams(vmem_limit_bytes=4 * 1024 * 1024),
+    )(departures, sums, jacobian)
+    return (departures, adjoint_t.transpose(1, 2, 0))
 
 
 def solution(mesh):

time: 34.6 us -> 29.3 us (0.85)
  local copies, waits for them, and re-layouts: 5.68 us -> 0.01 us
  Pallas kernels: 27.3 us -> 27.9 us
    unnamed x18 -> x2, local copies, waits for them, and re-layouts: 5.68 us -> 0.01 us
    pallas_call x0 -> x1, Pallas kernels: none -> 0.95 us  [body(): pl.pallas_call(finish_kernel, name='write_outputs', out_shape=(jax.ShapeD...]
    pallas_call x1, Pallas kernels: 27.3 us -> 26.9 us  [body(): pl.pallas_call(functools.partial(kernel, n_tm, n_space, chunks), name='de...]
where the time goes in v2:
time: 29.3 us; the launch traced here: 29.2 us
  Pallas kernels  27.9 us (95%)
  between operations  1.3 us (4%)
    pallas_call x1, Pallas kernels, body(): pl.pallas_call(functools.partial(kernel, n_tm, n_space, chunks), name='de...  26.9 us
    pallas_call x1, Pallas kernels, body(): pl.pallas_call(finish_kernel, name='write_outputs', out_shape=(jax.ShapeD...  0.95 us

profile of v2, /device:TPU:0, one launch (start us, length us, event | category | flops | bytes accessed | tf_op | source)
XLA Modules:
  0.0 29.2 jit_solution(4867804319363854359)
XLA Ops:
  1.3 0.0 copy-start
  1.3 26.9 %departures_and_adjoint.1 = (f32[512,128]{1,0:T(8,128)S(1)}, bf16[2,128,256]{2,1,0:T(8,128)(2,1)S(1)}) custom-call(bf16[137,512]{1,0:T(8,128)(2,1)} %bitcast.9, s32[1,512]{1,0:T(1,128)} %bitcast.11, bf16[8,512]{1,0:T(8,128)(2,1)} %bitcast.10, s32[1,512]{1,0:T(1,128)} %bitcast.12, f32[1,512]{1,0:T(1,128)} %bitcast.13, s32[1,1]{1,0:T(1,128)S(6)} %copy.11.live_ref, ...), custom_call_target="tpu_custom_call" | custom-call | tf_op jit(solution)/shard_map/departures_and_adjoint/pallas_call | solution.py:349
  28.2 0.0 copy-done
  28.2 1.0 %write_outputs.1 = (f32[512,128]{1,0:T(8,128)}, f32[137,1,512]{2,1,0:T(1,128)}) custom-call(f32[512,128]{1,0:T(8,128)S(1)} %get-tuple-element.6.dep_ref, bf16[2,128,256]{2,1,0:T(8,128)(2,1)S(1)} %get-tuple-element.7.sum_ref, bf16[137,128]{1,0:T(8,128)(2,1)S(1)} %copy-done), custom_call_target="tpu_custom_call" | custom-call | tf_op jit(solution)/shard_map/write_outputs/pallas_call | solution.py:401
Async XLA Ops:
  1.3 26.9 %copy-start = (bf16[137,128]{1,0:T(8,128)(2,1)S(1)}, bf16[137,128]{1,0:T(8,128)(2,1)}, u32[]{:S(2)}) copy-start(bf16[137,128]{1,0:T(8,128)(2,1)} %jac_ref.1) | copy-start | bytes 105220

commit v3 on v2

--- a/solution.py
+++ b/solution.py
@@ -26,11 +26,11 @@
     ny = n_tm // CORES
     names = [("meta_i", r) for r in range(1, n_tm)]
     names += [("meta_f", r) for r in range(1, n_tm)]
-    names += [("halo", side) for side in range(2)]
+    names += [("halo", k, side) for k in range(chunks) for side in range(2)]
     names += [("pair", dy, k) for dy in range(ny) for k in range(chunks)]
     names += [("sum", dy, k) for dy in range(1, ny) for k in range(chunks)]
     names += [("scaled", r, k) for r in range(1, n_tm) for k in range(chunks)]
-    names += [("rim", side) for side in range(2)]
+    names += [("rim", k, side) for k in range(chunks) for side in range(2)]
     return {name: index for index, name in enumerate(names)}
 
 
@@ -88,7 +88,6 @@
     halo_w = cols_dev // 2
     width = cols_dev + 2 * halo_w
     foot, obs = weight_ref.shape
-    chunk_w = obs // chunks
     names = message_names(n_tm, chunks)
 
     def peer(r):
@@ -146,16 +145,16 @@
             device_id_type=MESH,
         ).wait_recv()
 
-    def send_sides(name, sources, targets_there, source_index, target_index):
+    def send_sides(name, k, sources, targets_there, source_index, target_index):
         odd = lax.rem(tile, 2)
         for side in (odd, 1 - odd):
             device = (turn, lax.rem(tile + n_space - 1 + 2 * side, n_space))
-            base = names[(name, 0)]
+            base = names[(name, k, 0)]
             send_at(
                 base + side,
                 base + 1 - side,
-                sources.at[source_index(side)],
-                targets_there.at[target_index(side)],
+                sources.at[source_index(side), k],
+                targets_there.at[target_index(side), k],
                 device,
             )
 
@@ -181,11 +180,14 @@
     ).astype(F32).astype(BF16)
     jac_t = nt_dot(eye, jac).astype(BF16)
     own = nn_dot(jac_t, state_ref[...]).astype(BF16)
-    wide[1] = own[:, :halo_w]
-    wide[2] = own[:, halo_w:]
+    rows = chan // chunks
+    for k in range(chunks):
+        wide[1, k] = own[k * rows : (k + 1) * rows, :halo_w]
+        wide[2, k] = own[k * rows : (k + 1) * rows, halo_w:]
 
     pl.semaphore_wait(barrier, len(targets))
-    send_sides("halo", wide, wide, lambda side: 1 + side, lambda side: 3 - 3 * side)
+    for k in range(chunks):
+        send_sides("halo", k, wide, wide, lambda side: 1 + side, lambda side: 3 - 3 * side)
     for r in range(1, n_tm):
         back = inverse(r)
         send(("meta_i", r), ("meta_i", back), meta_i.at[0], meta_i.at[back], peer(r))
@@ -208,7 +210,7 @@
             foot_t[r, j * GROUP : (j + 1) * GROUP, :] = block
 
     def project(r, b):
-        return nn_dot(wide[b], foot_t[r, b * halo_w : (b + 1) * halo_w, :])
+        return nn_dot(wide[b].reshape(chan, halo_w), foot_t[r, b * halo_w : (b + 1) * halo_w, :])
 
     build(0)
     partial[0] = project(0, 1) + project(0, 2)
@@ -223,43 +225,50 @@
         build(r)
         partial[r] = project(r, 1) + project(r, 2)
 
-    arrived(("halo", 0), wide.at[0], (turn, left))
-    arrived(("halo", 1), wide.at[3], (turn, right))
-
     def finish(r, k):
-        lanes = slice(k * chunk_w, (k + 1) * chunk_w)
-        edge = nn_dot(wide[0], foot_t[r, 0:halo_w, lanes])
-        edge = edge + nn_dot(wide[3], foot_t[r, width - halo_w :, lanes])
-        return partial[r, :, lanes] + edge
-
-    for dy in range(1, ny):
-        for k in range(chunks):
-            pair_out[dy, k] = finish(dy * CORES + 1, k).astype(BF16)
-            send(("pair", dy, k), ("pair", dy, k), pair_out.at[dy, k], pair_in.at[dy, k], peer(1))
-    for dy in range(1, ny):
-        back = ny - dy
-        for k in range(chunks):
-            mine = finish(dy * CORES, k)
+        edge = nn_dot(wide[0, k], foot_t[r, 0:halo_w, :])
+        edge = edge + nn_dot(wide[3, k], foot_t[r, width - halo_w :, :])
+        partial[r, k * rows : (k + 1) * rows, :] += edge
+        return partial[r, k * rows : (k + 1) * rows, :]
+
+    def send_pair(dy, k):
+        pair_out[dy, k] = finish(dy * CORES + 1, k).astype(BF16)
+        send(("pair", dy, k), ("pair", dy, k), pair_out.at[dy, k], pair_in.at[dy, k], peer(1))
+
+    def send_sum(k):
+        for dy in range(1, ny):
+            back = ny - dy
             arrived(("pair", dy, k), pair_in.at[dy, k], peer(1))
+            mine = partial[dy * CORES, k * rows : (k + 1) * rows, :]
             sum_out[dy, k] = (mine + pair_in[dy, k].astype(F32)).astype(BF16)
             send(("sum", dy, k), ("sum", back, k), sum_out.at[dy, k], sum_in.at[back, k], peer(dy * CORES))
-    for k in range(chunks):
-        pair_out[0, k] = finish(1, k).astype(BF16)
-        send(("pair", 0, k), ("pair", 0, k), pair_out.at[0, k], pair_in.at[0, k], peer(1))
-    for k in range(chunks):
-        lanes = slice(k * chunk_w, (k + 1) * chunk_w)
-        partial[0, :, lanes] = finish(0, k)
-    for k in range(chunks):
-        lanes = slice(k * chunk_w, (k + 1) * chunk_w)
+
+    for k in range(chunks):
+        arrived(("halo", k, 0), wide.at[0, k], (turn, left))
+        arrived(("halo", k, 1), wide.at[3, k], (turn, right))
+        for dy in range(1, ny):
+            send_pair(dy, k)
+        for dy in range(1, ny):
+            finish(dy * CORES, k)
+        if k > 0:
+            send_sum(k - 1)
+    send_sum(chunks - 1)
+    for k in range(chunks):
+        send_pair(0, k)
+    for k in range(chunks):
+        finish(0, k)
+
+    for k in range(chunks):
+        part = slice(k * rows, (k + 1) * rows)
         arrived(("pair", 0, k), pair_in.at[0, k], peer(1))
-        projected = partial[0, :, lanes] + pair_in[0, k].astype(F32)
+        projected = partial[0, part, :] + pair_in[0, k].astype(F32)
         for dy in range(1, ny):
             arrived(("sum", dy, k), sum_in.at[dy, k], peer(dy * CORES))
             projected = projected + sum_in[dy, k].astype(F32)
-        place = lax.broadcasted_iota(jnp.int32, (chan, chunk_w), 1) + k * chunk_w
-        departure = jnp.where(place < live_ref[0, 0], values_t[:, lanes] - projected, 0.0)
-        dep_t[:, lanes] = departure
-        scale = jnp.concatenate([inv_t[...]] * (chunk_w // GROUP), axis=1)
+        place = lax.broadcasted_iota(jnp.int32, (rows, obs), 1)
+        departure = jnp.where(place < live_ref[0, 0], values_t[part, :] - projected, 0.0)
+        dep_t[part, :] = departure
+        scale = jnp.concatenate([inv_t[part, :]] * (obs // GROUP), axis=1)
         scaled[0, k] = (departure * scale).astype(BF16)
         for dy in range(1, ny):
             r = dy * CORES
@@ -268,22 +277,31 @@
         send(("scaled", 1, k), ("scaled", 1, k), scaled.at[0, k], scaled.at[1, k], peer(1))
 
     def spread(r, k, b):
-        lanes = slice(k * chunk_w, (k + 1) * chunk_w)
-        return nt_dot(scaled[r, k], foot_t[r, b * halo_w : (b + 1) * halo_w, lanes])
-
-    dep_ref[...] = dep_t[...].T
+        return nt_dot(scaled[r, k], foot_t[r, b * halo_w : (b + 1) * halo_w, :])
+
+    def spread_all(r, b):
+        return nt_dot(scaled[r].reshape(chan, obs), foot_t[r, b * halo_w : (b + 1) * halo_w, :])
+
     for b in range(4):
-        here = spread(0, 0, b)
-        for k in range(1, chunks):
-            here = here + spread(0, k, b)
-        total[b] = here
+        total[b] = spread_all(0, b)
     for k in range(chunks):
         arrived(("scaled", 1, k), scaled.at[1, k], peer(1))
     for b in range(4):
-        here = total[b]
-        for k in range(chunks):
-            here = here + spread(1, k, b)
-        total[b] = here
+        total[b] += spread_all(1, b)
+
+    def last(k, b):
+        here = total[b, k * rows : (k + 1) * rows, :]
+        for dy in range(1, ny):
+            here = here + spread(dy * CORES + 1, k, b)
+        return here
+
+    def send_rims(k):
+        for dy in range(1, ny):
+            arrived(("scaled", dy * CORES + 1, k), scaled.at[dy * CORES + 1, k], peer(1))
+        rim_out[0, k] = last(k, 0).astype(BF16)
+        rim_out[1, k] = last(k, 3).astype(BF16)
+        send_sides("rim", k, rim_out, rim_in, lambda side: side, lambda side: 1 - side)
+
     for k in range(chunks):
         for dy in range(1, ny):
             r = dy * CORES
@@ -291,25 +309,19 @@
             send(("scaled", r + 1, k), ("scaled", r + 1, k), scaled.at[r, k], scaled.at[r + 1, k], peer(1))
         for dy in range(1, ny):
             for b in range(4):
-                total[b] = total[b] + spread(dy * CORES, k, b)
-    for dy in range(1, ny):
+                total[b, k * rows : (k + 1) * rows, :] += spread(dy * CORES, k, b)
+        if k > 0:
+            send_rims(k - 1)
+    send_rims(chunks - 1)
+    for b in (1, 2):
+        for dy in range(1, ny):
+            total[b] += spread_all(dy * CORES + 1, b)
+    dep_ref[...] = dep_t[...].T
+    for side in range(2):
         for k in range(chunks):
-            arrived(("scaled", dy * CORES + 1, k), scaled.at[dy * CORES + 1, k], peer(1))
-
-    def last(b):
-        here = total[b]
-        for dy in range(1, ny):
-            for k in range(chunks):
-                here = here + spread(dy * CORES + 1, k, b)
-        return here
-
-    rim_out[0] = last(0).astype(BF16)
-    rim_out[1] = last(3).astype(BF16)
-    send_sides("rim", rim_out, rim_in, lambda side: side, lambda side: 1 - side)
-    core_sums = [last(1), last(2)]
-    for side in range(2):
-        arrived(("rim", side), rim_in.at[side], (turn, (left, right)[side]))
-        sum_ref[side] = (core_sums[side] + rim_in[side].astype(F32)).astype(BF16)
+            arrived(("rim", k, side), rim_in.at[side, k], (turn, (left, right)[side]))
+        rim = rim_in[side].reshape(chan, halo_w).astype(F32)
+        sum_ref[side] = (total[1 + side] + rim).astype(BF16)
     for copy in started:
         copy.wait_send()
 
@@ -335,13 +347,13 @@
     n_tm = lax.axis_size("tm")
     n_space = lax.axis_size("space")
     ny = n_tm // CORES
-    chunks = 4
+    chunks = 2
     _, cols_dev, levels = state.shape
     obs, chan = obs_values.shape
     foot = foot_weight.shape[1]
     halo_w = cols_dev // 2
     width = cols_dev + 2 * halo_w
-    chunk_w = obs // chunks
+    rows = chan // chunks
     vmem = pl.BlockSpec(memory_space=pltpu.VMEM)
     live_space = pl.BlockSpec(memory_space=pltpu.SMEM)
     hbm = pl.BlockSpec(memory_space=pltpu.HBM)
@@ -364,21 +376,21 @@
             pltpu.VMEM((obs, chan), F32),
             pltpu.VMEM((levels, chan), BF16),
             pltpu.VMEM((1, chan), F32),
-            pltpu.VMEM((4, chan, halo_w), BF16),
+            pltpu.VMEM((4, chunks, rows, halo_w), BF16),
             pltpu.VMEM((n_tm, 2, obs), jnp.int32),
             pltpu.VMEM((n_tm, 2 * foot, obs), BF16),
             pltpu.VMEM((n_tm, width, obs), BF16),
             pltpu.VMEM((n_tm, chan, obs), F32),
             pltpu.VMEM((chan, obs), F32),
             pltpu.VMEM((chan, GROUP), F32),
-            pltpu.VMEM((ny, chunks, chan, chunk_w), BF16),
-            pltpu.VMEM((ny, chunks, chan, chunk_w), BF16),
-            pltpu.VMEM((ny, chunks, chan, chunk_w), BF16),
-            pltpu.VMEM((ny, chunks, chan, chunk_w), BF16),
-            pltpu.VMEM((n_tm, chunks, chan, chunk_w), BF16),
+            pltpu.VMEM((ny, chunks, rows, obs), BF16),
+            pltpu.VMEM((ny, chunks, rows, obs), BF16),
+            pltpu.VMEM((ny, chunks, rows, obs), BF16),
+            pltpu.VMEM((ny, chunks, rows, obs), BF16),
+            pltpu.VMEM((n_tm, chunks, rows, obs), BF16),
             pltpu.VMEM((4, chan, halo_w), F32),
-            pltpu.VMEM((2, chan, halo_w), BF16),
-            pltpu.VMEM((2, chan, halo_w), BF16),
+            pltpu.VMEM((2, chunks, rows, halo_w), BF16),
+            pltpu.VMEM((2, chunks, rows, halo_w), BF16),
             pltpu.VMEM((chan, obs), F32),
             pltpu.SemaphoreType.DMA((8,)),
             pltpu.SemaphoreType.DMA((count,)),

time: 29.3 us -> 28.4 us (0.969)
  Pallas kernels: 27.9 us -> 27 us
    pallas_call x1, Pallas kernels: 26.9 us -> 26 us  [body(): pl.pallas_call(functools.partial(kernel, n_tm, n_space, chunks), name='de...]
where the time goes in v3:
time: 28.4 us; the launch traced here: 28.3 us
  Pallas kernels  27 us (95%)
  between operations  1.3 us (5%)
    pallas_call x1, Pallas kernels, body(): pl.pallas_call(functools.partial(kernel, n_tm, n_space, chunks), name='de...  26 us
    pallas_call x1, Pallas kernels, body(): pl.pallas_call(finish_kernel, name='write_outputs', out_shape=(jax.ShapeD...  0.95 us

profile of v3, /device:TPU:0, one launch (start us, length us, event | category | flops | bytes accessed | tf_op | source)
XLA Modules:
  0.0 28.3 jit_solution(14414931119683196919)
XLA Ops:
  1.3 0.0 copy-start
  1.3 26.0 %departures_and_adjoint.1 = (f32[512,128]{1,0:T(8,128)S(1)}, bf16[2,128,256]{2,1,0:T(8,128)(2,1)S(1)}) custom-call(bf16[137,512]{1,0:T(8,128)(2,1)} %bitcast.9, s32[1,512]{1,0:T(1,128)} %bitcast.11, bf16[8,512]{1,0:T(8,128)(2,1)} %bitcast.10, s32[1,512]{1,0:T(1,128)} %bitcast.12, f32[1,512]{1,0:T(1,128)} %bitcast.13, s32[1,1]{1,0:T(1,128)S(6)} %copy.11.live_ref, ...), custom_call_target="tpu_custom_call" | custom-call | tf_op jit(solution)/shard_map/departures_and_adjoint/pallas_call | solution.py:361
  27.3 0.0 copy-done
  27.3 1.0 %write_outputs.1 = (f32[512,128]{1,0:T(8,128)}, f32[137,1,512]{2,1,0:T(1,128)}) custom-call(f32[512,128]{1,0:T(8,128)S(1)} %get-tuple-element.6.dep_ref, bf16[2,128,256]{2,1,0:T(8,128)(2,1)S(1)} %get-tuple-element.7.sum_ref, bf16[137,128]{1,0:T(8,128)(2,1)S(1)} %copy-done), custom_call_target="tpu_custom_call" | custom-call | tf_op jit(solution)/shard_map/write_outputs/pallas_call | solution.py:413
Async XLA Ops:
  1.3 26.0 %copy-start = (bf16[137,128]{1,0:T(8,128)(2,1)S(1)}, bf16[137,128]{1,0:T(8,128)(2,1)}, u32[]{:S(2)}) copy-start(bf16[137,128]{1,0:T(8,128)(2,1)} %jac_ref.1) | copy-start | bytes 105220
